TPU v7x, 128 devices: a whole 4x4x4 slice. The times are simulated.
128 devices in a mesh: task: 8 (over x_hi, z), dp: 16 (over x_lo, y, core).
Axes of the slice: x: 4 (x_hi: 2, x_lo: 2; x = x_hi * 2 + x_lo), y: 4, z: 4, core: 2. Of those that a mesh axis runs over, the one named last changes fastest.
Arguments:
- tokens_in: bfloat16 [131072, 4096], P(('task', 'dp')), may hold values from -45 to 45
- query_cotangent: bfloat16 [131072, 2048], P(('task', 'dp')), may hold values from -23040 to 23040
- task_index: int32 [131072], P(('task', 'dp')), may hold values from 0 to 15, as said below
- loss_weights: int32 [16], replicated, may hold values from 1 to 4
- master: float32 [4096, 2048], P(('task', 'dp')), may hold values from -6 to 6
- moment_first: float32 [4096, 2048], P(('task', 'dp')), may hold values from -6 to 6
- moment_second: float32 [4096, 2048], P(('task', 'dp')), may hold values from 0.05 to 5
Outputs:
- new_master: float32 [4096, 2048], P(('task', 'dp'))
- new_first: float32 [4096, 2048], P(('task', 'dp'))
- new_second: float32 [4096, 2048], P(('task', 'dp'))
Inputs may be any that keep to these rules, and one draw needn't show every extreme that they name: `task_index`: the first 16 tokens name each task once.
All inputs are finite; a program needn't handle non-finite values.
Results may differ from a plain program's by a relative error of at most 0.00042.
Values may be sent and summed in bfloat16 or wider, within the bound.
A program may use at most 192 MiB of HBM per device.

v0:
```python
import jax
import jax.numpy as jnp
from jax import lax
from jax.sharding import Mesh
from jax.sharding import PartitionSpec as P

D = 4096
QW = 2048
TASK_DP = ("task_0", "task_1", "dp_0", "dp_1", "dp_2")
TASK = ("task_0", "task_1")
DP = ("dp_0", "dp_1", "dp_2")
beta_one = 0.9
beta_two = 0.95
adam_eps = 1e-08
step_rate = 0.01
decay_rate = 0.1
corr_one = 1.0 - 0.9**10
corr_two = 1.0 - 0.95**10


def over_axes(value, axes):
    for axis in axes:
        value = lax.psum(value, axis)
    return value


def split_up(value, dim, size):
    shape = value.shape
    blocks = value.reshape(*shape[:dim], size, shape[dim] // size, *shape[dim + 1 :])
    return jnp.moveaxis(blocks, dim, 0)


def summed_on_arrival(value, axis, dim):
    blocks = split_up(value, dim, lax.axis_size(axis))
    arrived = lax.all_to_all(blocks, axis, split_axis=0, concat_axis=0, tiled=True)
    return arrived.sum(axis=0)


def shards(
    tokens_in, query_cotangent, task_index, loss_weights, master, moment_first, moment_second
):
    labels = lax.iota(jnp.int32, loss_weights.shape[0])
    member = task_index[:, None] == labels[None, :]
    local_counts = jnp.sum(member.astype(jnp.int32), axis=0)
    counts = over_axes(local_counts, TASK_DP)
    task_scale = loss_weights.astype(jnp.float32) / counts.astype(jnp.float32)
    token_scale = jnp.sum(jnp.where(member, task_scale[None, :], jnp.float32(0.0)), axis=1)
    weighted = (query_cotangent.astype(jnp.float32) * token_scale[:, None]).astype(jnp.bfloat16)
    out_rows = master.shape[0]
    feature_count = weighted.shape[1]
    group_count = lax.axis_size(TASK)
    lane_count = lax.axis_size(DP)
    arranged = tokens_in.reshape(tokens_in.shape[0], group_count, lane_count, out_rows)
    group_rows = group_count * out_rows
    products = jnp.einsum("ntdr,nq->dtrq", arranged, weighted, preferred_element_type=jnp.float32)
    partial_value = lax.psum_scatter(
        products.reshape(lax.axis_size(DP) * group_rows, feature_count),
        DP,
        scatter_dimension=0,
        tiled=True,
    )
    gradient = summed_on_arrival(partial_value, TASK, 0)
    square_sum = over_axes(jnp.sum(gradient * gradient), TASK_DP)
    root_mean = jnp.sqrt(square_sum / (D * QW))
    factor = 1.0 / jnp.maximum(root_mean, 1.0)
    clipped = gradient * factor
    new_first = beta_one * moment_first + (1.0 - beta_one) * clipped
    new_second = beta_two * moment_second + (1.0 - beta_two) * clipped * clipped
    direction = new_first / corr_one / (jnp.sqrt(new_second / corr_two) + adam_eps)
    new_master = master - step_rate * (direction + decay_rate * master)
    return (new_master, new_first, new_second)


def solution(mesh):
    finer = Mesh(mesh.devices.reshape(2, 4, 2, 4, 2), ("task_0", "task_1", "dp_0", "dp_1", "dp_2"))
    in_specs = (
        P(TASK_DP, None),
        P(TASK_DP, None),
        P(TASK_DP),
        P(),
        P(TASK_DP, None),
        P(TASK_DP, None),
        P(TASK_DP, None),
    )
    out_specs = (P(TASK_DP, None), P(TASK_DP, None), P(TASK_DP, None))
    return jax.shard_map(
        shards, mesh=finer, in_specs=in_specs, out_specs=out_specs, check_vma=False
    )
```

profile of v0, /device:TPU:1, one launch (start us, length us, event | category | flops | bytes accessed | tf_op | source)
XLA Modules:
  0.0 349.0 jit_solution(1351179126321543253)
XLA Ops:
  7.2 0.0 reduce-scatter.2.cloned.1.call-start
  7.2 0.8 convert_reduce_fusion
  8.0 5.2 %psum.70 = s32[16]{0:T(128)S(1)} all-reduce(s32[16]{0:T(128)S(1)} %convert_reduce_fusion), channel_id=1, replica_groups=mesh['task_0'=2,'task_1'=4,'dp_0'=2,'dp_1'=4,'dp_2'=2] {'task_0'}, use_global_device_ids=true, to_apply=%region_1.0 | all-reduce | flops 16 | bytes 128 | tf_op jit(solution)/shard_map/psum | solution.py:23
  13.3 7.9 %psum.71 = s32[16]{0:T(128)S(1)} all-reduce(s32[16]{0:T(128)S(1)} %psum.70), channel_id=1, replica_groups=mesh['task_0'=2,'task_1'=4,'dp_0'=2,'dp_1'=4,'dp_2'=2] {'task_1'}, use_global_device_ids=true, to_apply=%region_2.0 | all-reduce | flops 16 | bytes 128 | tf_op jit(solution)/shard_map/psum | solution.py:23
  21.2 3.4 psum.72
  24.6 7.0 %psum.73 = s32[16]{0:T(128)S(1)} all-reduce(s32[16]{0:T(128)S(1)} %psum.72), channel_id=1, replica_groups=mesh['task_0'=2,'task_1'=4,'dp_0'=2,'dp_1'=4,'dp_2'=2] {'dp_1'}, use_global_device_ids=true, to_apply=%region_4.0 | all-reduce | flops 16 | bytes 128 | tf_op jit(solution)/shard_map/psum | solution.py:23
  31.6 8.2 %psum.74 = s32[16]{0:T(128)S(1)} all-reduce(s32[16]{0:T(128)S(1)} %psum.73), channel_id=1, replica_groups=mesh['task_0'=2,'task_1'=4,'dp_0'=2,'dp_1'=4,'dp_2'=2] {'dp_2'}, use_global_device_ids=true, to_apply=%region_5.0 | all-reduce | flops 16 | bytes 128 | tf_op jit(solution)/shard_map/psum | solution.py:23
  39.8 0.7 convert_divide_fusion
  40.4 0.8 select_reduce_fusion
  41.2 26.0 %fusion = f32[2048,4096]{0,1} fusion(bf16[1024,4096]{1,0:T(8,128)(2,1)} %param.7, bf16[1024,2048]{1,0:T(8,128)(2,1)} %param.8, f32[1024]{0:T(1024)S(1)} %select_reduce_fusion), kind=kOutput, calls=%fused_computation.1 | convolution fusion | flops 17186160640 | bytes 46141440
  67.2 23.0 %copy.14 = f32[16,8,32,2048]{3,2,1,0:T(8,128)} copy(f32[16,8,32,2048]{3,2,0,1:T(8,128)} %bitcast.10) | data formatting | bytes 67108864 | tf_op jit(solution)/shard_map/ntdr,nq->dtrq/transpose | solution.py:55
  90.2 0.0 reduce-scatter.2.cloned.1.call-update
  90.3 178.2 %reduce-scatter.2.cloned.1.call-done = f32[256,2048]{1,0:T(8,128)} async-done(((f32[4096,2048]{1,0:T(8,128)}), f32[256,2048]{1,0:T(8,128)}) %reduce-scatter.2.cloned.1.call-update) | async-done | bytes 2097168 | tf_op jit(solution)/shard_map/reduce_scatter | solution.py:56
  268.5 32.0 %all_to_all.5 = f32[8,32,2048]{2,1,0:T(8,128)S(1)} all-to-all(f32[8,32,2048]{2,1,0:T(8,128)} %bitcast.11), channel_id=1, replica_groups=mesh['task_0'=2,'task_1'=4,'dp_0'=2,'dp_1'=4,'dp_2'=2] {'task_0','task_1'}, dimensions={0} | all-to-all | bytes 4194304 | tf_op jit(solution)/shard_map/all_to_all | solution.py:35
  300.5 0.1 reduce_sum.38
  300.6 0.7 multiply_reduce_fusion
  301.2 5.9 %psum.75 = f32[]{:T(128)} all-reduce(f32[]{:T(128)} %multiply_reduce_fusion), channel_id=1, replica_groups=mesh['task_0'=2,'task_1'=4,'dp_0'=2,'dp_1'=4,'dp_2'=2] {'task_0'}, use_global_device_ids=true, to_apply=%region_10.11 | all-reduce | flops 1 | bytes 8 | tf_op jit(solution)/shard_map/psum | solution.py:23
  307.1 7.9 %psum.76 = f32[]{:T(128)} all-reduce(f32[]{:T(128)} %psum.75), channel_id=1, replica_groups=mesh['task_0'=2,'task_1'=4,'dp_0'=2,'dp_1'=4,'dp_2'=2] {'task_1'}, use_global_device_ids=true, to_apply=%region_11.12 | all-reduce | flops 1 | bytes 8 | tf_op jit(solution)/shard_map/psum | solution.py:23
  315.0 4.4 %psum.77 = f32[]{:T(128)} all-reduce(f32[]{:T(128)} %psum.76), channel_id=1, replica_groups=mesh['task_0'=2,'task_1'=4,'dp_0'=2,'dp_1'=4,'dp_2'=2] {'dp_0'}, use_global_device_ids=true, to_apply=%region_12.13 | all-reduce | flops 1 | bytes 8 | tf_op jit(solution)/shard_map/psum | solution.py:23
  319.4 11.5 %psum.78 = f32[]{:T(128)} all-reduce(f32[]{:T(128)} %psum.77), channel_id=1, replica_groups=mesh['task_0'=2,'task_1'=4,'dp_0'=2,'dp_1'=4,'dp_2'=2] {'dp_1'}, use_global_device_ids=true, to_apply=%region_13.14 | all-reduce | flops 1 | bytes 8 | tf_op jit(solution)/shard_map/psum | solution.py:23
  330.9 9.5 %psum.79 = f32[]{:T(128)} all-reduce(f32[]{:T(128)} %psum.78), channel_id=1, replica_groups=mesh['task_0'=2,'task_1'=4,'dp_0'=2,'dp_1'=4,'dp_2'=2] {'dp_2'}, use_global_device_ids=true, to_apply=%region_14.15 | all-reduce | flops 1 | bytes 8 | tf_op jit(solution)/shard_map/psum | solution.py:23
  341.1 0.0 copy-done
  341.2 0.0 copy-done.1
  341.2 1.0 multiply_subtract_fusion
  (4 shorter events, 0.0 us)
Async XLA Ops:
  7.2 261.3 %reduce-scatter.2.cloned.1.call-start = ((), (), s32[]{:S(2)}) async-start(), calls=%async_computation.2 | async-start | bytes 35651584 | tf_op jit(solution)/shard_map/reduce_scatter | solution.py:56
  90.2 250.9 %copy-start = (f32[32,2048]{1,0:T(8,128)S(1)}, f32[32,2048]{1,0:T(8,128)}, u32[]{:S(2)}) copy-start(f32[32,2048]{1,0:T(8,128)} %param.11) | copy-start | bytes 786436
  90.2 250.9 %copy-start.1 = (f32[32,2048]{1,0:T(8,128)S(1)}, f32[32,2048]{1,0:T(8,128)}, u32[]{:S(2)}) copy-start(f32[32,2048]{1,0:T(8,128)} %param.12) | copy-start | bytes 786436
  90.2 250.9 %copy-start.2 = (f32[32,2048]{1,0:T(8,128)S(1)}, f32[32,2048]{1,0:T(8,128)}, u32[]{:S(2)}) copy-start(f32[32,2048]{1,0:T(8,128)} %param.13) | copy-start | bytes 786436
Sparse Core Ops, SparseCore 0:
  90.4 178.0 reduce-scatter.1
where the time goes:
time: 350 us; the launch traced here: 349 us
  waiting for transfers between devices  178 us (51%)
  blocking collectives  103 us (29%)
  matrix products  26 us (7%)
  local copies, waits for them, and re-layouts  23 us (7%)
  between operations  14.8 us (4%)
  other arithmetic  4.03 us (1%)
    reduce_scatter x1, waiting for transfers between devices, shards(): lax.psum_scatter(products.reshape(lax.axis_size(DP) * group_rows, feature...  178 us
    psum x10, blocking collectives, over_axes(): value = lax.psum(value, axis)  70.9 us
    all_to_all x1, blocking collectives, summed_on_arrival(): lax.all_to_all(blocks, axis, split_axis=0, concat_axis=0, tiled=True)  32 us
    unnamed x1, matrix products  26 us
    transpose x1, local copies, waits for them, and re-layouts, shards(): jnp.einsum('ntdr,nq->dtrq', arranged, weighted, preferred_element_type=jn...  23 us
  transfers between devices with their start and end apart: 1, of which 1 were waited for; matrix products, arithmetic and copies ran while one was open for 0% of the time, Pallas kernels for 0%

commit v1 on v0

--- a/solution.py
+++ b/solution.py
@@ -20,7 +20,7 @@
 
 def over_axes(value, axes):
     for axis in axes:
-        value = lax.psum(value, axis)
+        value = jnp.sum(lax.all_gather(value, axis), axis=0)
     return value
 
 

time: 350 us -> 368 us (1.051)
  blocking collectives: 103 us -> 67.4 us
  waiting for transfers between devices: 178 us -> 204 us
  local copies, waits for them, and re-layouts: 23 us -> 38 us
  starting transfers between devices: 0.04 us -> 6.62 us
    psum x10 -> x0, blocking collectives: 70.9 us -> none  [over_axes(): value = lax.psum(value, axis)]
    unnamed x0 -> x10, blocking collectives: none -> 67.4 us
    all_to_all x1 -> x0, blocking collectives: 32 us -> none  [summed_on_arrival(): lax.all_to_all(blocks, axis, split_axis=0, concat_axis=0, tiled=True)]
    all_to_all x0 -> x1, waiting for transfers between devices: none -> 26.2 us  [summed_on_arrival(): lax.all_to_all(blocks, axis, split_axis=0, concat_axis=0, tiled=True)]
    unnamed x6 -> x31, local copies, waits for them, and re-layouts: 0.01 us -> 14.5 us
    all_to_all x0 -> x1, starting transfers between devices: none -> 6.58 us  [summed_on_arrival(): lax.all_to_all(blocks, axis, split_axis=0, concat_axis=0, tiled=True)]
  transfers between devices with their start and end apart: 1 -> 2, of which waited for: 1 -> 2; matrix products, arithmetic and copies ran while one was open for 0% -> 0% of each run, Pallas kernels for 0% -> 0%
where the time goes in v1:
time: 368 us
  waiting for transfers between devices  204 us (55%)
  blocking collectives  67.4 us (18%)
  local copies, waits for them, and re-layouts  38 us (10%)
  matrix products  26 us (7%)
  between operations  18.1 us (5%)
  other arithmetic  7.23 us (2%)
  starting transfers between devices  6.62 us (2%)
    reduce_scatter x1, waiting for transfers between devices, shards(): lax.psum_scatter(products.reshape(lax.axis_size(DP) * group_rows, feature...  178 us
    unnamed x10, blocking collectives  67.4 us
    all_to_all x1, waiting for transfers between devices, summed_on_arrival(): lax.all_to_all(blocks, axis, split_axis=0, concat_axis=0, tiled=True)  26.2 us
    unnamed x1, matrix products  26 us
    transpose x1, local copies, waits for them, and re-layouts, shards(): jnp.einsum('ntdr,nq->dtrq', arranged, weighted, preferred_element_type=jn...  23 us
    unnamed x31, local copies, waits for them, and re-layouts  14.5 us
  transfers between devices with their start and end apart: 2, of which 2 were waited for; matrix products, arithmetic and copies ran while one was open for 0% of the time, Pallas kernels for 0%

profile of v1, /device:TPU:1, one launch (start us, length us, event | category | flops | bytes accessed | tf_op | source)
XLA Modules:
  0.0 367.6 jit_solution(13079426077619168313)
XLA Ops:
  8.0 1.2 dynamic-slice
  10.2 5.2 %all-reduce = s32[32]{0:T(128)S(1)} all-reduce(s32[32]{0:T(128)S(1)} %dynamic-update-slice), channel_id=2, replica_groups=mesh['task_0'=2,'task_1'=4,'dp_0'=2,'dp_1'=4,'dp_2'=2] {'task_0'}, use_global_device_ids=true, to_apply=%add | all-reduce | flops 32 | bytes 256
  15.5 1.2 dynamic-slice.1
  17.6 7.9 %all-reduce.1 = s32[64]{0:T(128)S(1)} all-reduce(s32[64]{0:T(128)S(1)} %dynamic-update-slice.1), channel_id=3, replica_groups=mesh['task_0'=2,'task_1'=4,'dp_0'=2,'dp_1'=4,'dp_2'=2] {'task_1'}, use_global_device_ids=true, to_apply=%add.1 | all-reduce | flops 64 | bytes 512
  25.6 1.2 dynamic-slice.2
  27.8 3.1 all-reduce.2
  33.1 7.0 %all-reduce.3 = s32[64]{0:T(128)S(1)} all-reduce(s32[64]{0:T(128)S(1)} %dynamic-update-slice.3), channel_id=5, replica_groups=mesh['task_0'=2,'task_1'=4,'dp_0'=2,'dp_1'=4,'dp_2'=2] {'dp_1'}, use_global_device_ids=true, to_apply=%add.3 | all-reduce | flops 64 | bytes 512
  40.2 1.3 dynamic-slice.4
  42.5 8.5 %all-reduce.4 = s32[32]{0:T(128)S(1)} all-reduce(s32[32]{0:T(128)S(1)} %dynamic-update-slice.4), channel_id=6, replica_groups=mesh['task_0'=2,'task_1'=4,'dp_0'=2,'dp_1'=4,'dp_2'=2] {'dp_2'}, use_global_device_ids=true, to_apply=%add.4 | all-reduce | flops 32 | bytes 256
  52.5 26.0 %fusion = f32[2048,4096]{0,1} fusion(bf16[1024,4096]{1,0:T(8,128)(2,1)} %param.7, bf16[1024,2048]{1,0:T(8,128)(2,1)} %param.8, f32[1024]{0:T(1024)S(1)} %select_reduce_fusion), kind=kOutput, calls=%fused_computation.1 | convolution fusion | flops 17186160640 | bytes 46141440
  78.5 23.0 %copy.14 = f32[16,8,32,2048]{3,2,1,0:T(8,128)} copy(f32[16,8,32,2048]{3,2,0,1:T(8,128)} %bitcast.25) | data formatting | bytes 67108864 | tf_op jit(solution)/shard_map/ntdr,nq->dtrq/transpose | solution.py:55
  101.5 178.2 %reduce-scatter.2.cloned.1.call-done = f32[256,2048]{1,0:T(8,128)} async-done(((f32[4096,2048]{1,0:T(8,128)}), f32[256,2048]{1,0:T(8,128)}) %reduce-scatter.2.cloned.1.call-update) | async-done | bytes 2097168 | tf_op jit(solution)/shard_map/reduce_scatter | solution.py:56
  279.7 6.6 %all-to-all-start = ((f32[8,32,2048]{2,1,0:T(8,128)}), f32[8,32,2048]{2,1,0:T(8,128)S(1)}, u32[]{:S(2)}, u32[]{:S(2)}) async-start(f32[8,32,2048]{2,1,0:T(8,128)} %bitcast.26), calls=%async_computation.1 | async-start | bytes 4194304 | tf_op jit(solution)/shard_map/all_to_all | solution.py:35
  286.3 26.2 %all-to-all-done = f32[8,32,2048]{2,1,0:T(8,128)S(1)} async-done(((f32[8,32,2048]{2,1,0:T(8,128)}), f32[8,32,2048]{2,1,0:T(8,128)S(1)}, u32[]{:S(2)}, u32[]{:S(2)}) %all-to-all-start) | async-done | bytes 2097184 | tf_op jit(solution)/shard_map/all_to_all | solution.py:35
  313.3 1.4 dynamic-update-slice.5
  314.8 5.3 %all-reduce.5 = f32[2]{0:T(128)S(1)} all-reduce(f32[2]{0:T(128)S(1)} %dynamic-update-slice.5), channel_id=1, replica_groups=mesh['task_0'=2,'task_1'=4,'dp_0'=2,'dp_1'=4,'dp_2'=2] {'task_0'}, use_global_device_ids=true, to_apply=%add.5 | all-reduce | flops 2 | bytes 16
  320.7 1.4 dynamic-update-slice.6
  322.1 7.2 %all-reduce.6 = f32[4]{0:T(128)S(1)} all-reduce(f32[4]{0:T(128)S(1)} %dynamic-update-slice.6), channel_id=1, replica_groups=mesh['task_0'=2,'task_1'=4,'dp_0'=2,'dp_1'=4,'dp_2'=2] {'task_1'}, use_global_device_ids=true, to_apply=%add.6 | all-reduce | flops 4 | bytes 32
  329.8 1.4 dynamic-update-slice.7
  331.2 3.8 %all-reduce.7 = f32[2]{0:T(128)S(1)} all-reduce(f32[2]{0:T(128)S(1)} %dynamic-update-slice.7), channel_id=1, replica_groups=mesh['task_0'=2,'task_1'=4,'dp_0'=2,'dp_1'=4,'dp_2'=2] {'dp_0'}, use_global_device_ids=true, to_apply=%add.7 | all-reduce | flops 2 | bytes 16
  335.6 1.3 dynamic-update-slice.8
  336.9 10.6 %all-reduce.8 = f32[4]{0:T(128)S(1)} all-reduce(f32[4]{0:T(128)S(1)} %dynamic-update-slice.8), channel_id=1, replica_groups=mesh['task_0'=2,'task_1'=4,'dp_0'=2,'dp_1'=4,'dp_2'=2] {'dp_1'}, use_global_device_ids=true, to_apply=%add.8 | all-reduce | flops 4 | bytes 32
  348.1 1.4 dynamic-update-slice.9
  349.5 8.9 %all-reduce.9 = f32[2]{0:T(128)S(1)} all-reduce(f32[2]{0:T(128)S(1)} %dynamic-update-slice.9), channel_id=1, replica_groups=mesh['task_0'=2,'task_1'=4,'dp_0'=2,'dp_1'=4,'dp_2'=2] {'dp_2'}, use_global_device_ids=true, to_apply=%add.9 | all-reduce | flops 2 | bytes 16
  (45 shorter events, 10.2 us)
Async XLA Ops:
  7.2 272.5 %reduce-scatter.2.cloned.1.call-start = ((), (), s32[]{:S(2)}) async-start(), calls=%async_computation.2 | async-start | bytes 35651584 | tf_op jit(solution)/shard_map/reduce_scatter | solution.py:56
  101.5 258.3 %copy-start = (f32[32,2048]{1,0:T(8,128)S(1)}, f32[32,2048]{1,0:T(8,128)}, u32[]{:S(2)}) copy-start(f32[32,2048]{1,0:T(8,128)} %param.11) | copy-start | bytes 786436
  101.5 258.3 %copy-start.1 = (f32[32,2048]{1,0:T(8,128)S(1)}, f32[32,2048]{1,0:T(8,128)}, u32[]{:S(2)}) copy-start(f32[32,2048]{1,0:T(8,128)} %param.12) | copy-start | bytes 786436
  101.5 258.3 %copy-start.2 = (f32[32,2048]{1,0:T(8,128)S(1)}, f32[32,2048]{1,0:T(8,128)}, u32[]{:S(2)}) copy-start(f32[32,2048]{1,0:T(8,128)} %param.13) | copy-start | bytes 786436
  279.7 32.8 %all-to-all-start = ((f32[8,32,2048]{2,1,0:T(8,128)}), f32[8,32,2048]{2,1,0:T(8,128)S(1)}, u32[]{:S(2)}, u32[]{:S(2)}) async-start(f32[8,32,2048]{2,1,0:T(8,128)} %bitcast.26), calls=%async_computation.1 | async-start | bytes 4194304 | tf_op jit(solution)/shard_map/all_to_all | solution.py:35
Sparse Core Ops, SparseCore 0:
  101.6 178.0 reduce-scatter.1
